TPU v7x, 32 devices: a whole 2x2x4 slice. The times are simulated.
32 devices in a mesh: ctx: 8 (over z, core), head: 4 (over y, x).
Axes of the slice: x: 2, y: 2, z: 4, core: 2. Of those that a mesh axis runs over, the one named last changes fastest.
Arguments:
- queries: bfloat16 [2048, 8192], P(('ctx', 'head')), may hold values from -100 to 100
- keys: bfloat16 [2048, 1024], P(('ctx', 'head')), may hold values from -100 to 100
- values: bfloat16 [2048, 1024], P(('ctx', 'head')), may hold values from -6 to 6
- out_grad: bfloat16 [2048, 8192], P(('ctx', 'head')), may hold values from -6 to 6
- doc_ids: int32 [2048], replicated, may hold values from 0 to 3, never falling along the last dimension, each value on 1 to 1024 neighbouring positions
Outputs:
- query_grad: float32 [2048, 8192], P(('ctx', 'head'))
- key_grad: float32 [2048, 1024], P(('ctx', 'head'))
- value_grad: float32 [2048, 1024], P(('ctx', 'head'))
Inputs may be any that keep to these rules, and one draw needn't show every extreme that they name: `doc_ids`: never falling along the sequence; each document holds 1 to 1024 tokens, one exactly 1024.
All inputs are finite; a program needn't handle non-finite values.
Results may differ from a plain program's by a relative error of at most 0.004.
Values may be sent and summed in bfloat16 or wider, within the bound.
A program may use at most 64 MiB of HBM per device.

v0:
```python
import functools
import math
import jax
import jax.numpy as jnp
from jax import lax
from jax.experimental import pallas as pl
from jax.experimental.pallas import tpu as pltpu
from jax.sharding import PartitionSpec as P

HD = 128
BACK = 3
CHUNK = 4
MESH = pl.DeviceIdType.MESH
NT = (((1,), (1,)), ((), ()))


def kernel(
    n_ctx, n_head, group,
    q_ref, k_ref, v_ref, g_ref, doc_ref,
    dq_out, dk_out, dv_out,
    q_buf, g_buf, dq_buf, kv_buf, kt_buf, acc, bias, part_out, part_in, own_part, tot,
    own_sem, kv_send, kv_recv, ctx_send, ctx_recv, in_send, in_recv,
    dq_send, dq_recv, part_send, part_recv, tot_send, tot_recv,
):
    c = lax.axis_index("ctx")
    h = lax.axis_index("head")
    rows = q_ref.shape[0]
    blk = rows * n_head
    kv_n = kv_buf.shape[0]
    n_chunk, _, width = q_buf.shape
    per_kv = n_chunk // kv_n
    cols = n_chunk * width
    scale = 1.0 / HD**0.5
    spread = range(1, BACK + 1)

    def peer(p):
        other, bit = 0, 1
        while bit < n_head:
            other = other + ((h // bit) % 2 + (p // bit) % 2) % 2 * bit
            bit *= 2
        return other

    barrier = pltpu.get_barrier_semaphore()
    for p in range(1, n_head):
        pl.semaphore_signal(barrier, inc=1, device_id=(c, peer(p)), device_id_type=MESH)
    for s in spread:
        for to in ((c + s) % n_ctx, (c - s + n_ctx) % n_ctx):
            pl.semaphore_signal(barrier, inc=1, device_id=(to, h), device_id_type=MESH)
    pl.semaphore_wait(barrier, n_head - 1 + 2 * BACK)

    def at(n, size):
        return pl.ds(pl.multiple_of(n * size, size), size)

    def kv_copy(kv, t, p):
        to = peer(p)
        ref = (k_ref, v_ref)[t]
        return pltpu.make_async_remote_copy(
            src_ref=ref.at[:, at(to * kv_n + kv, HD)],
            dst_ref=kv_buf.at[kv, BACK, t, at(h, rows)],
            send_sem=kv_send.at[kv, t, p - 1],
            recv_sem=kv_recv.at[kv, t, p - 1],
            device_id=(c, to), device_id_type=MESH,
        )

    def kv_own(kv, t):
        ref = (k_ref, v_ref)[t]
        return pltpu.make_async_copy(
            ref.at[:, at(h * kv_n + kv, HD)], kv_buf.at[kv, BACK, t, at(h, rows)],
            own_sem.at[kv, t],
        )

    def in_copy(ch, t, p):
        to = peer(p)
        return pltpu.make_async_remote_copy(
            src_ref=(q_ref, g_ref)[t].at[:, at(to * n_chunk + ch, width)],
            dst_ref=(q_buf, g_buf)[t].at[ch, at(h, rows)],
            send_sem=in_send.at[ch, t, p - 1],
            recv_sem=in_recv.at[ch, t, p - 1],
            device_id=(c, to), device_id_type=MESH,
        )

    def in_own(ch, t):
        return pltpu.make_async_copy(
            (q_ref, g_ref)[t].at[:, at(h * n_chunk + ch, width)],
            (q_buf, g_buf)[t].at[ch, at(h, rows)],
            in_recv.at[ch, t, n_head - 1],
        )

    def ctx_copy(kv, s):
        return pltpu.make_async_remote_copy(
            src_ref=kv_buf.at[kv, BACK], dst_ref=kv_buf.at[kv, BACK - s],
            send_sem=ctx_send.at[kv, s - 1], recv_sem=ctx_recv.at[kv, s - 1],
            device_id=((c + s) % n_ctx, h), device_id_type=MESH,
        )

    def dq_copy(ch, p):
        to = peer(p)
        return pltpu.make_async_remote_copy(
            src_ref=dq_buf.at[ch, at(to, rows)],
            dst_ref=dq_out.at[:, at(h * n_chunk + ch, width)],
            send_sem=dq_send.at[ch, p - 1], recv_sem=dq_recv.at[ch, p - 1],
            device_id=(c, to), device_id_type=MESH,
        )

    def dq_own(ch):
        return pltpu.make_async_copy(
            dq_buf.at[ch, at(h, rows)], dq_out.at[:, at(h * n_chunk + ch, width)],
            dq_send.at[ch, n_head - 1],
        )

    def part_copy(kv, s):
        return pltpu.make_async_remote_copy(
            src_ref=part_out.at[kv, s - 1], dst_ref=part_in.at[kv, s - 1],
            send_sem=part_send.at[kv, s - 1], recv_sem=part_recv.at[kv, s - 1],
            device_id=((c - s + n_ctx) % n_ctx, h), device_id_type=MESH,
        )

    def tot_copy(kv, t, p):
        to = peer(p)
        return pltpu.make_async_remote_copy(
            src_ref=tot.at[kv, t, at(to, rows)],
            dst_ref=(dk_out, dv_out)[t].at[:, at(h * kv_n + kv, HD)],
            send_sem=tot_send.at[kv, t, p - 1], recv_sem=tot_recv.at[kv, t, p - 1],
            device_id=(c, to), device_id_type=MESH,
        )

    def tot_own(kv, t):
        return pltpu.make_async_copy(
            tot.at[kv, t, at(h, rows)], (dk_out, dv_out)[t].at[:, at(h * kv_n + kv, HD)],
            tot_send.at[kv, t, n_head - 1],
        )

    others = range(1, n_head)
    for kv in range(kv_n):
        for t in range(2):
            for p in others:
                kv_copy(kv, t, p).start()
            kv_own(kv, t).start()

    @pl.loop(0, n_chunk)
    def _(ch):
        for t in range(2):
            for p in others:
                in_copy(ch, t, p).start()
            in_own(ch, t).start()

    for kv in range(kv_n):
        for t in range(2):
            kv_own(kv, t).wait()
            for p in others:
                kv_copy(kv, t, p).wait_recv()
        for s in spread:
            @pl.when(c + s < n_ctx)
            def _():
                ctx_copy(kv, s).start()

            @pl.when(c < s)
            def _():
                kv_buf[kv, BACK - s] = jnp.zeros(kv_buf.shape[2:], kv_buf.dtype)

    tile = HD
    query_doc = doc_ref[:, pl.ds(pl.multiple_of(c * blk, blk), blk)].astype(jnp.float32)
    for part in range(4 * blk // tile):
        key_blk = jnp.maximum(c - BACK + part * tile // blk, 0)
        start = pl.multiple_of(key_blk * blk + part * tile % blk, tile)
        key_row = doc_ref[:, pl.ds(start, tile)].astype(jnp.float32)
        key_doc = jnp.transpose(jnp.broadcast_to(key_row, (tile, tile)))
        key_doc = jnp.concatenate([key_doc] * (blk // tile), axis=1)
        j = lax.broadcasted_iota(jnp.int32, (tile, blk), 0) + part * tile
        i = lax.broadcasted_iota(jnp.int32, (tile, blk), 1)
        ok = (j > i) & (j <= i + BACK * blk) & (j + (c - BACK) * blk >= 0)
        ok = ok & (key_doc == query_doc)
        bias[pl.ds(part * tile, tile)] = jnp.where(ok, 0.0, -1e30)

    for kv in range(kv_n):
        for s in spread:
            @pl.when(c >= s)
            def _():
                ctx_copy(kv, s).wait_recv()

        keys = kv_buf[kv, :, 0].reshape(4 * blk, HD)
        kt_buf[...] = jnp.transpose(keys.astype(jnp.float32)).astype(jnp.bfloat16)
        acc[...] = jnp.zeros(acc.shape, acc.dtype)

        @pl.loop(0, per_kv)
        def _(step):
            ch = kv * per_kv + step
            for t in range(2):
                in_own(ch, t).wait()
                for p in others:
                    in_copy(ch, t, p).wait_recv()
            for a in range(width // HD):
                lanes = pl.ds(a * HD, HD)
                q = q_buf[ch, :, lanes]
                g = g_buf[ch, :, lanes]
                key_win = kv_buf[kv, :, 0].reshape(4 * blk, HD)
                val_win = kv_buf[kv, :, 1].reshape(4 * blk, HD)
                s_t = lax.dot_general(key_win, q, NT, preferred_element_type=jnp.float32)
                s_t = s_t + bias[...]
                top = jnp.max(s_t, axis=0, keepdims=True)
                e_t = jnp.exp2((s_t - top) * (scale * math.log2(math.e)))
                w_t = e_t * (1.0 / jnp.sum(e_t, axis=0, keepdims=True))
                w_bf = w_t.astype(jnp.bfloat16)
                p_t = lax.dot_general(val_win, g, NT, preferred_element_type=jnp.float32)
                delta = jnp.sum(w_bf.astype(jnp.float32) * p_t, axis=0, keepdims=True)
                d_t = (w_t * (p_t - delta)).astype(jnp.bfloat16)
                dv = jnp.dot(w_bf, g, preferred_element_type=jnp.float32)
                dk = jnp.dot(d_t, q, preferred_element_type=jnp.float32)
                acc[:, 0] += dk.reshape(4, blk, HD)
                acc[:, 1] += dv.reshape(4, blk, HD)
                dq_t = jnp.dot(kt_buf[...], d_t, preferred_element_type=jnp.float32)
                dq_buf[ch, :, lanes] = jnp.transpose(dq_t * scale).astype(jnp.bfloat16)
            for p in others:
                dq_copy(ch, p).start()
            dq_own(ch).start()

        for s in spread:
            part_out[kv, s - 1, 0] = (acc[BACK - s, 0] * scale).astype(jnp.bfloat16)
            part_out[kv, s - 1, 1] = acc[BACK - s, 1].astype(jnp.bfloat16)

            @pl.when(c >= s)
            def _():
                part_copy(kv, s).start()
        own_part[kv, 0] = acc[BACK, 0] * scale
        own_part[kv, 1] = acc[BACK, 1]

    for kv in range(kv_n):
        for s in spread:
            @pl.when(c + s < n_ctx)
            def _():
                part_copy(kv, s).wait_recv()
                own_part[kv] += part_in[kv, s - 1].astype(jnp.float32)

        tot[kv] = own_part[kv].astype(jnp.bfloat16)
        for t in range(2):
            for p in others:
                tot_copy(kv, t, p).start()
            tot_own(kv, t).start()

    @pl.loop(0, n_chunk)
    def _(ch):
        for t in range(2):
            for p in others:
                in_copy(ch, t, p).wait_send()
        for p in others:
            dq_copy(ch, p).wait()
        dq_own(ch).wait()

    for kv in range(kv_n):
        for t in range(2):
            for p in others:
                kv_copy(kv, t, p).wait_send()
                tot_copy(kv, t, p).wait()
            tot_own(kv, t).wait()
        for s in spread:
            @pl.when(c + s < n_ctx)
            def _():
                ctx_copy(kv, s).wait_send()

            @pl.when(c >= s)
            def _():
                part_copy(kv, s).wait_send()


def body(queries, keys, values, out_grad, doc_ids):
    n_ctx, n_head = lax.axis_size("ctx"), lax.axis_size("head")
    rows, q_cols = queries.shape
    kv_cols = keys.shape[1]
    blk = rows * n_head
    kv_n = kv_cols // HD // n_head
    group = q_cols // kv_cols
    chunk = math.gcd(CHUNK, group)
    width = chunk * HD
    n_chunk = kv_n * group // chunk
    win = BACK + 1
    bf, f32, dma = jnp.bfloat16, jnp.float32, pltpu.SemaphoreType.DMA
    far = pl.BlockSpec(memory_space=pl.ANY)
    near = pl.BlockSpec(memory_space=pltpu.VMEM)
    dq, dk, dv = pl.pallas_call(
        functools.partial(kernel, n_ctx, n_head, group),
        out_shape=(
            jax.ShapeDtypeStruct((rows, q_cols), bf),
            jax.ShapeDtypeStruct((rows, kv_cols), bf),
            jax.ShapeDtypeStruct((rows, kv_cols), bf),
        ),
        in_specs=[far, far, far, far, near],
        out_specs=(far, far, far),
        scratch_shapes=[
            pltpu.VMEM((n_chunk, blk, width), bf),
            pltpu.VMEM((n_chunk, blk, width), bf),
            pltpu.VMEM((n_chunk, blk, width), bf),
            pltpu.VMEM((kv_n, win, 2, blk, HD), bf),
            pltpu.VMEM((HD, win * blk), bf),
            pltpu.VMEM((win, 2, blk, HD), f32),
            pltpu.VMEM((win * blk, blk), f32),
            pltpu.VMEM((kv_n, BACK, 2, blk, HD), bf),
            pltpu.VMEM((kv_n, BACK, 2, blk, HD), bf),
            pltpu.VMEM((kv_n, 2, blk, HD), f32),
            pltpu.VMEM((kv_n, 2, blk, HD), bf),
            dma((kv_n, 2)),
            dma((kv_n, 2, n_head)),
            dma((kv_n, 2, n_head)),
            dma((kv_n, BACK)),
            dma((kv_n, BACK)),
            dma((n_chunk, 2, n_head)),
            dma((n_chunk, 2, n_head)),
            dma((n_chunk, n_head)),
            dma((n_chunk, n_head)),
            dma((kv_n, BACK)),
            dma((kv_n, BACK)),
            dma((kv_n, 2, n_head)),
            dma((kv_n, 2, n_head)),
        ],
        compiler_params=pltpu.CompilerParams(
            collective_id=0, has_side_effects=True, vmem_limit_bytes=56 * 2**20
        ),
    )(queries, keys, values, out_grad, doc_ids.reshape(1, -1))
    return dq.astype(f32), dk.astype(f32), dv.astype(f32)


def solution(mesh):
    split = P(("ctx", "head"), None)
    return jax.shard_map(
        body,
        mesh=mesh,
        in_specs=(split, split, split, split, P()),
        out_specs=(split, split, split),
        check_vma=False,
    )
```

profile of v0, /device:TPU:1, one launch (start us, length us, event | category | flops | bytes accessed | tf_op | source)
XLA Modules:
  0.0 59.4 jit_solution(9515440484294877549)
XLA Ops:
  0.6 54.6 %shard_map.76 = (bf16[64,8192]{1,0:T(8,128)(2,1)}, bf16[64,1024]{1,0:T(8,128)(2,1)}, bf16[64,1024]{1,0:T(8,128)(2,1)}) custom-call(bf16[64,8192]{1,0:T(8,128)(2,1)} %q_ref.1, bf16[64,1024]{1,0:T(8,128)(2,1)} %k_ref.1, bf16[64,1024]{1,0:T(8,128)(2,1)} %v_ref.1, bf16[64,8192]{1,0:T(8,128)(2,1)} %g_ref.1, s32[1,2048]{1,0:T(1,128)} %bitcast.1), custom_call_target="tpu_custom_call" | custom-call | tf_op jit(solution)/shard_map/pallas_call | solution.py:279
  55.2 0.0 copy-start.1
  55.2 0.0 copy-start
  55.2 2.7 %convert_element_type.9 = f32[64,8192]{1,0:T(8,128)} convert(bf16[64,8192]{1,0:T(8,128)(2,1)} %get-tuple-element.6) | non-fusion elementwise | flops 524288 | bytes 3145728 | tf_op jit(solution)/shard_map/convert_element_type | solution.py:318
  57.9 0.0 copy-done.1
  57.9 0.7 %convert_element_type.10 = f32[64,1024]{1,0:T(8,128)} convert(bf16[64,1024]{1,0:T(8,128)(2,1)S(1)} %copy-done.1) | non-fusion elementwise | flops 65536 | bytes 393216 | tf_op jit(solution)/shard_map/convert_element_type | solution.py:318
  58.7 0.0 copy-done
  58.7 0.7 %convert_element_type.11 = f32[64,1024]{1,0:T(8,128)} convert(bf16[64,1024]{1,0:T(8,128)(2,1)S(1)} %copy-done) | non-fusion elementwise | flops 65536 | bytes 393216 | tf_op jit(solution)/shard_map/convert_element_type | solution.py:318
Async XLA Ops:
  55.2 2.7 %copy-start.1 = (bf16[64,1024]{1,0:T(8,128)(2,1)S(1)}, bf16[64,1024]{1,0:T(8,128)(2,1)}, u32[]{:S(2)}) copy-start(bf16[64,1024]{1,0:T(8,128)(2,1)} %get-tuple-element.7) | copy-start | bytes 393220
  55.2 3.5 %copy-start = (bf16[64,1024]{1,0:T(8,128)(2,1)S(1)}, bf16[64,1024]{1,0:T(8,128)(2,1)}, u32[]{:S(2)}) copy-start(bf16[64,1024]{1,0:T(8,128)(2,1)} %get-tuple-element.8) | copy-start | bytes 393220
where the time goes:
time: 59.6 us; the launch traced here: 59.4 us
  Pallas kernels  54.6 us (92%)
  other arithmetic  4.16 us (7%)
  between operations  0.66 us (1%)
    pallas_call x1, Pallas kernels, body(): pl.pallas_call(functools.partial(kernel, n_ctx, n_head, group), out_shape...  54.6 us
    convert_element_type x3, other arithmetic, body(): return (dq.astype(f32), dk.astype(f32), dv.astype(f32))  4.16 us

commit v1 on v0

v1 whole, which is shorter than its diff:
```python
import functools
import math
import jax
import jax.numpy as jnp
from jax import lax
from jax.experimental import pallas as pl
from jax.experimental.pallas import tpu as pltpu
from jax.sharding import PartitionSpec as P

HD = 128
BACK = 3
SLOTS = 4
MESH = pl.DeviceIdType.MESH
NT = (((1,), (1,)), ((), ()))


def flip(v, mask):
    bit = 1
    while bit <= mask:
        if mask & bit:
            v = v + bit * (1 - 2 * ((v // bit) % 2))
        bit *= 2
    return v


def kernel(
    n_ctx, n_head,
    q_ref, k_ref, v_ref, g_ref, doc_ref,
    dq_out, dk_out, dv_out,
    q_buf, g_buf, dq_buf, kv_buf, kt_buf, acc, bias, part_out, part_in, tot_out, tot_in,
    kv_send, kv_recv, in_send, in_recv, up_send, up_recv, last_send, last_recv,
    dq_send, dq_recv, part_send, part_recv, tot_send, tot_recv,
):
    c = lax.axis_index("ctx")
    h = lax.axis_index("head")
    k = c % 2
    z = c // 2
    n_z = n_ctx // 2
    rows = q_ref.shape[0]
    blk = rows * n_head
    jobs, _, n_st, pair, width = q_buf.shape
    heads = width // HD
    scale = 1.0 / HD**0.5
    has_up, has_down, has_two = z + 1 < n_z, z >= 1, z >= 2

    def at(n, size):
        return pl.ds(pl.multiple_of(n * size, size), size)

    def bit_of(v, j):
        return (v // (1 << j % 2)) % 2

    def dev(dk, dh):
        return (flip(c, dk), flip(h, dh))

    mine = [2 * bit_of(h, j) + k for j in range(jobs)]
    plane = [(dk, dh) for dh in range(n_head) for dk in range(2)]
    others = plane[1:]
    up = ((c + 2) % n_ctx, h)
    down = ((c - 2 + n_ctx) % n_ctx, h)

    barrier = pltpu.get_barrier_semaphore()
    for to in [dev(*p) for p in others] + [up, down]:
        pl.semaphore_signal(barrier, inc=1, device_id=to, device_id_type=MESH)
    pl.semaphore_wait(barrier, len(others) + 2)

    def kv_copy(j, t, p):
        dk, dh = p
        slot = 2 * bit_of(flip(h, dh), j) + flip(k, dk)
        src = (k_ref, v_ref)[t].at[:, at(SLOTS * j + slot, HD)]
        dst = kv_buf.at[j, BACK + k, t, at(h, rows)]
        if p == (0, 0):
            return pltpu.make_async_copy(src, dst, kv_recv.at[j, t, 0, 0])
        return pltpu.make_async_remote_copy(
            src_ref=src, dst_ref=dst,
            send_sem=kv_send.at[j, t, dk, dh], recv_sem=kv_recv.at[j, t, dk, dh],
            device_id=dev(dk, dh), device_id_type=MESH,
        )

    def kv_arrived(j, p):
        for t in range(2):
            if p == (0, 0):
                kv_copy(j, t, p).wait()
            else:
                kv_copy(j, t, p).wait_recv()

    def in_copy(j, s, t, dk, db):
        slot = 2 * flip(bit_of(h, j), db) + flip(k, dk)
        src = (q_ref, g_ref)[t].at[:, at((SLOTS * j + slot) * n_st + s, width)]
        dst = (q_buf, g_buf)[t].at[j, k, s, at(bit_of(h, j), rows)]
        arrive = in_recv.at[j, s, t, k, bit_of(h, j)]
        if (dk, db) == (0, 0):
            return pltpu.make_async_copy(src, dst, arrive)
        return pltpu.make_async_remote_copy(
            src_ref=src, dst_ref=dst,
            send_sem=in_send.at[j, s, t, dk, db], recv_sem=arrive,
            device_id=dev(dk, db << j % 2), device_id_type=MESH,
        )

    def in_arrived(j, s, kk):
        for t in range(2):
            for b in range(2):
                dst = (q_buf, g_buf)[t].at[j, kk, s, pl.ds(b * rows, rows)]
                pltpu.make_async_copy(dst, dst, in_recv.at[j, s, t, kk, b]).wait()

    def up_copy(j, kk, dh):
        part = kv_buf.at[j, BACK + kk, :, at(flip(h, dh), rows)]
        return pltpu.make_async_remote_copy(
            src_ref=part, dst_ref=kv_buf.at[j, BACK + kk - 2, :, at(flip(h, dh), rows)],
            send_sem=up_send.at[j, kk, dh], recv_sem=up_recv.at[j, kk, dh],
            device_id=up, device_id_type=MESH,
        )

    def last_copy(j):
        return pltpu.make_async_remote_copy(
            src_ref=kv_buf.at[j, 2], dst_ref=kv_buf.at[j, 0],
            send_sem=last_send.at[j], recv_sem=last_recv.at[j],
            device_id=up, device_id_type=MESH,
        )

    def dq_copy(j, s, kk, b):
        src = dq_buf.at[j, kk, s, pl.ds(b * rows, rows)]
        dst = dq_out.at[:, at((SLOTS * j + mine[j]) * n_st + s, width)]
        arrive = dq_recv.at[j, s, k, bit_of(h, j)]
        shift = 1 << j % 2
        owner = h + shift * (b - bit_of(h, j))
        far = pltpu.make_async_remote_copy(
            src_ref=src, dst_ref=dst,
            send_sem=dq_send.at[j, s, kk, b], recv_sem=arrive,
            device_id=(2 * z + kk, owner), device_id_type=MESH,
        )
        own = pltpu.make_async_copy(src, dst, arrive)
        return far, own, (k == kk) & (bit_of(h, j) == b)

    def part_copy(j, m):
        return pltpu.make_async_remote_copy(
            src_ref=part_out.at[j, m], dst_ref=part_in.at[j, m],
            send_sem=part_send.at[j, m], recv_sem=part_recv.at[j, m],
            device_id=down, device_id_type=MESH,
        )

    def tot_copy(j, p):
        dk, dh = p
        return pltpu.make_async_remote_copy(
            src_ref=tot_out.at[j, flip(k, dk), :, at(flip(h, dh), rows)],
            dst_ref=tot_in.at[j, k, h],
            send_sem=tot_send.at[j, dk, dh], recv_sem=tot_recv.at[j, k, h],
            device_id=dev(dk, dh), device_id_type=MESH,
        )

    def start_kv(j):
        for p in plane:
            for t in range(2):
                kv_copy(j, t, p).start()

    def start_in(j, s):
        for db in range(2):
            for dk in range(2):
                for t in range(2):
                    in_copy(j, s, t, dk, db).start()

    start_kv(0)
    start_in(0, 0)
    for j in range(1, jobs):
        start_kv(j)
    for j in range(jobs):
        @pl.loop(1 if j == 0 else 0, n_st)
        def _(s):
            start_in(j, s)

    tile = HD
    lane = lax.broadcasted_iota(jnp.int32, (8, blk), 1)

    def make_bias(j, kk):
        shift = 1 << j % 2
        block = 2 * z + kk
        docs = jnp.broadcast_to(
            doc_ref[:, pl.ds(pl.multiple_of(block * blk, blk), blk)].astype(jnp.float32), (8, blk)
        )
        first = h - shift * bit_of(h, j)
        query_doc = jnp.zeros((8, blk), jnp.float32)
        for u in range(heads):
            for b in range(2):
                to = (2 * u + b) * rows
                turn = (to - (first + b * shift) * rows + 2 * blk) % blk
                query_doc = jnp.where(lane // rows == 2 * u + b, pltpu.roll(docs, turn, 1), query_doc)
        query_doc = query_doc[:1]
        col = lax.broadcasted_iota(jnp.int32, (tile, blk), 1)
        i = (first + (col // rows) % 2 * shift) * rows + col % rows
        for part in range(4 * blk // tile):
            key_blk = jnp.maximum(block - BACK + part * tile // blk, 0)
            start = pl.multiple_of(key_blk * blk + part * tile % blk, tile)
            key_row = doc_ref[:, pl.ds(start, tile)].astype(jnp.float32)
            key_doc = jnp.transpose(jnp.broadcast_to(key_row, (tile, tile)))
            key_doc = jnp.concatenate([key_doc] * (blk // tile), axis=1)
            row = lax.broadcasted_iota(jnp.int32, (tile, blk), 0) + part * tile
            ok = (row > i) & (row <= i + BACK * blk) & (row + (block - BACK) * blk >= 0)
            ok = ok & (key_doc == query_doc)
            bias[j, kk, pl.ds(part * tile, tile)] = jnp.where(ok, 0.0, -1e30)

    def gather_and_send_up(j):
        for dh in range(n_head):
            for dk in range(2):
                kv_arrived(j, (dk, dh))

            @pl.when(has_up)
            def _():
                for kk in (1, 0):
                    up_copy(j, kk, dh).start()

            yield

    def fill(j):
        @pl.when(z < 1)
        def _():
            kv_buf[j, 1:3] = jnp.zeros((2,) + kv_buf.shape[2:], kv_buf.dtype)

        @pl.when(z < 2)
        def _():
            kv_buf[j, 0] = jnp.zeros(kv_buf.shape[2:], kv_buf.dtype)

    def wait_down(j, kk):
        @pl.when(has_down)
        def _():
            for dh in range(n_head):
                up_copy(j, kk, dh).wait_recv()

    def hand_on(j):
        wait_down(j, 1)

        @pl.when(has_down & has_up)
        def _():
            last_copy(j).start()

    def wait_last(j):
        @pl.when(has_two)
        def _():
            last_copy(j).wait_recv()

    def turn_keys(j, first, last):
        keys = kv_buf[j, first:last, 0].reshape((last - first) * blk, HD)
        kt_buf[j, :, first * blk : last * blk] = jnp.transpose(keys.astype(jnp.float32)).astype(jnp.bfloat16)

    def attend(j, kk, s):
        in_arrived(j, s, kk)
        lanes = [slice(a * HD, (a + 1) * HD) for a in range(heads)]
        q = jnp.concatenate([q_buf[j, kk, s, :, a] for a in lanes], axis=0)
        g = jnp.concatenate([g_buf[j, kk, s, :, a] for a in lanes], axis=0)
        key_win = kv_buf[j, kk : kk + 4, 0].reshape(4 * blk, HD)
        val_win = kv_buf[j, kk : kk + 4, 1].reshape(4 * blk, HD)
        s_t = lax.dot_general(key_win, q, NT, preferred_element_type=jnp.float32)
        s_t = s_t + bias[j, kk]
        top = jnp.max(s_t, axis=0, keepdims=True)
        e_t = jnp.exp2((s_t - top) * (scale * math.log2(math.e)))
        w_t = e_t * (1.0 / jnp.sum(e_t, axis=0, keepdims=True))
        w_bf = w_t.astype(jnp.bfloat16)
        p_t = lax.dot_general(val_win, g, NT, preferred_element_type=jnp.float32)
        delta = jnp.sum(w_bf.astype(jnp.float32) * p_t, axis=0, keepdims=True)
        d_t = (w_t * (p_t - delta)).astype(jnp.bfloat16)
        dv = jnp.dot(w_bf, g, preferred_element_type=jnp.float32)
        dk = jnp.dot(d_t, q, preferred_element_type=jnp.float32)
        acc[j, kk : kk + 4, 0] += dk.reshape(4, blk, HD)
        acc[j, kk : kk + 4, 1] += dv.reshape(4, blk, HD)
        keys_t = kt_buf[j, :, kk * blk : (kk + 4) * blk]
        dq_t = jnp.dot(keys_t, d_t, preferred_element_type=jnp.float32)
        dq = jnp.transpose(dq_t * scale).astype(jnp.bfloat16)
        for n, a in enumerate(lanes):
            dq_buf[j, kk, s, :, a] = dq[n * pair : (n + 1) * pair]
        for b in range(2):
            far, own, here = dq_copy(j, s, kk, b)
            pl.when(jnp.logical_not(here))(far.start)
            pl.when(here)(own.start)

    def send_part(j, m, cond):
        part_out[j, m, 0] = (acc[j, m, 0] * scale).astype(jnp.bfloat16)
        part_out[j, m, 1] = acc[j, m, 1].astype(jnp.bfloat16)
        pl.when(cond)(part_copy(j, m).start)

    def add_part(j, m, cond):
        @pl.when(cond)
        def _():
            part_copy(j, m).wait_recv()
            acc[j, m + 2, 0] += part_in[j, m, 0].astype(jnp.float32) * (1.0 / scale)
            acc[j, m + 2, 1] += part_in[j, m, 1].astype(jnp.float32)

    def send_tot(j):
        for kk in range(2):
            add_part(j, kk + 1, has_up)
            tot_out[j, kk, 0] = (acc[j, BACK + kk, 0] * scale).astype(jnp.bfloat16)
            tot_out[j, kk, 1] = acc[j, BACK + kk, 1].astype(jnp.bfloat16)
        for p in others:
            tot_copy(j, p).start()
        tot_in[j, k, h] = tot_out[j, k, :, at(h, rows)]

    def send_mid(j):
        add_part(j, 0, has_up & has_down)
        send_part(j, 2, has_down)

    for j in range(jobs):
        fill(j)
        acc[j] = jnp.zeros(acc.shape[1:], acc.dtype)
    chores = [functools.partial(make_bias, j, kk) for j in range(jobs) for kk in (1, 0)]
    for _ in gather_and_send_up(0):
        if chores:
            chores.pop(0)()
    for chore in chores:
        chore()
    hand_on(0)

    for j in range(jobs):
        final = j == jobs - 1
        if j == 0:
            wait_down(0, 0)
            turn_keys(0, 1, 5)

            @pl.loop(0, n_st)
            def _(s):
                attend(0, 1, s)

                @pl.when(s == 0)
                def _():
                    if not final:
                        for _ in gather_and_send_up(1):
                            pass
                    wait_last(0)
                    turn_keys(0, 0, 1)

                attend(0, 0, s)

                if not final:
                    @pl.when(s == n_st // 2)
                    def _():
                        hand_on(1)
        else:
            wait_down(j, 0)
            wait_last(j)
            turn_keys(j, 0, 5)

            @pl.loop(0, n_st)
            def _(s):
                attend(j, 0, s)

                @pl.when(s == 0)
                def _():
                    send_mid(j - 1)
                    if not final:
                        for _ in gather_and_send_up(j + 1):
                            pass

            send_part(j, 0, has_two)

            @pl.loop(0, n_st)
            def _(s):
                attend(j, 1, s)

                @pl.when(s == 0)
                def _():
                    send_tot(j - 1)
                    if not final:
                        hand_on(j + 1)

        if j == 0:
            send_part(j, 0, has_two)
        send_part(j, 1, has_down)
        if final:
            send_mid(j)
            send_tot(j)

    for j in range(jobs):
        for b in range(2):
            for kk in range(2):
                n = SLOTS * j + 2 * b + kk
                for t in range(2):
                    total = jnp.zeros((rows, HD), jnp.float32)
                    for hh in range(n_head):
                        if (hh >> j % 2) & 1 == b:
                            if t == 0:
                                @pl.when((k != kk) | (h != hh))
                                def _():
                                    got = tot_in.at[j, kk, hh]
                                    pltpu.make_async_copy(got, got, tot_recv.at[j, kk, hh]).wait()
                            total = total + tot_in[j, kk, hh, t].astype(jnp.float32)
                    (dk_out, dv_out)[t][:, n * HD : (n + 1) * HD] = total

    for j in range(jobs):
        @pl.loop(0, n_st)
        def _(s):
            for dk in range(2):
                for b in range(2):
                    if (dk, b) != (0, 0):
                        for t in range(2):
                            in_copy(j, s, t, dk, b).wait_send()
                    far, own, here = dq_copy(j, s, dk, b)
                    pl.when(jnp.logical_not(here))(far.wait_send)
                    got = dq_buf.at[j, dk, s, pl.ds(b * rows, rows)]
                    pltpu.make_async_copy(got, got, dq_recv.at[j, s, dk, b]).wait()

        for p in others:
            for t in range(2):
                kv_copy(j, t, p).wait_send()
            tot_copy(j, p).wait_send()

        @pl.when(has_up)
        def _():
            for kk in range(2):
                for dh in range(n_head):
                    up_copy(j, kk, dh).wait_send()

        pl.when(has_up & has_down)(last_copy(j).wait_send)
        pl.when(has_two)(part_copy(j, 0).wait_send)
        pl.when(has_down)(part_copy(j, 1).wait_send)
        pl.when(has_down)(part_copy(j, 2).wait_send)


def body(queries, keys, values, out_grad, doc_ids):
    n_ctx, n_head = lax.axis_size("ctx"), lax.axis_size("head")
    rows, q_cols = queries.shape
    kv_cols = keys.shape[1]
    blk = rows * n_head
    jobs = kv_cols // HD // SLOTS
    group = q_cols // kv_cols
    heads = n_head // 2
    n_st = group // heads
    pair = 2 * rows
    win = BACK + 2
    bf, f32, dma = jnp.bfloat16, jnp.float32, pltpu.SemaphoreType.DMA
    far = pl.BlockSpec(memory_space=pl.ANY)
    near = pl.BlockSpec(memory_space=pltpu.VMEM)
    dq, dk, dv = pl.pallas_call(
        functools.partial(kernel, n_ctx, n_head),
        out_shape=(
            jax.ShapeDtypeStruct((rows, q_cols), bf),
            jax.ShapeDtypeStruct((rows, kv_cols), f32),
            jax.ShapeDtypeStruct((rows, kv_cols), f32),
        ),
        in_specs=[far, far, far, far, near],
        out_specs=(far, near, near),
        scratch_shapes=[
            pltpu.VMEM((jobs, 2, n_st, pair, heads * HD), bf),
            pltpu.VMEM((jobs, 2, n_st, pair, heads * HD), bf),
            pltpu.VMEM((jobs, 2, n_st, pair, heads * HD), bf),
            pltpu.VMEM((jobs, win, 2, blk, HD), bf),
            pltpu.VMEM((jobs, HD, win * blk), bf),
            pltpu.VMEM((jobs, win, 2, blk, HD), f32),
            pltpu.VMEM((jobs, 2, 4 * blk, blk), f32),
            pltpu.VMEM((jobs, 3, 2, blk, HD), bf),
            pltpu.VMEM((jobs, 3, 2, blk, HD), bf),
            pltpu.VMEM((jobs, 2, 2, blk, HD), bf),
            pltpu.VMEM((jobs, 2, n_head, 2, rows, HD), bf),
            dma((jobs, 2, 2, n_head)),
            dma((jobs, 2, 2, n_head)),
            dma((jobs, n_st, 2, 2, 2)),
            dma((jobs, n_st, 2, 2, 2)),
            dma((jobs, 2, n_head)),
            dma((jobs, 2, n_head)),
            dma((jobs,)),
            dma((jobs,)),
            dma((jobs, n_st, 2, 2)),
            dma((jobs, n_st, 2, 2)),
            dma((jobs, 3)),
            dma((jobs, 3)),
            dma((jobs, 2, n_head)),
            dma((jobs, 2, n_head)),
        ],
        compiler_params=pltpu.CompilerParams(
            collective_id=0, has_side_effects=True, vmem_limit_bytes=56 * 2**20
        ),
    )(queries, keys, values, out_grad, doc_ids.reshape(1, -1))
    return dq.astype(f32), dk, dv


def solution(mesh):
    split = P(("ctx", "head"), None)
    return jax.shard_map(
        body,
        mesh=mesh,
        in_specs=(split, split, split, split, P()),
        out_specs=(split, split, split),
        check_vma=False,
    )
```

time: 59.6 us -> 65.7 us (1.10)
  Pallas kernels: 54.6 us -> 60.3 us
  other arithmetic: 4.16 us -> 2.74 us
  local copies, waits for them, and re-layouts: 0.01 us -> 1.41 us
    pallas_call x1, Pallas kernels: 54.6 us -> 60.3 us  [body(): pl.pallas_call(functools.partial(kernel, n_ctx, n_head), out_shape=(jax.S...]
    convert_element_type x3 -> x1, other arithmetic: 4.16 us -> 2.74 us  [body(): return (dq.astype(f32), dk, dv)]
    unnamed x4 -> x6, local copies, waits for them, and re-layouts: 0.01 us -> 1.41 us
where the time goes in v1:
time: 65.7 us; the launch traced here: 65.2 us
  Pallas kernels  60.3 us (92%)
  other arithmetic  2.74 us (4%)
  local copies, waits for them, and re-layouts  1.41 us (2%)
  between operations  0.66 us (1%)
    pallas_call x1, Pallas kernels, body(): pl.pallas_call(functools.partial(kernel, n_ctx, n_head), out_shape=(jax.S...  60.3 us
    convert_element_type x1, other arithmetic, body(): return (dq.astype(f32), dk, dv)  2.74 us
    unnamed x6, local copies, waits for them, and re-layouts  1.41 us

profile of v1, /device:TPU:1, one launch (start us, length us, event | category | flops | bytes accessed | tf_op | source)
XLA Modules:
  0.0 65.2 jit_solution(1546612715350383687)
XLA Ops:
  0.6 60.3 %shard_map.76 = (bf16[64,8192]{1,0:T(8,128)(2,1)}, f32[64,1024]{1,0:T(8,128)}, f32[64,1024]{1,0:T(8,128)}) custom-call(bf16[64,8192]{1,0:T(8,128)(2,1)} %q_ref.1, bf16[64,1024]{1,0:T(8,128)(2,1)} %k_ref.1, bf16[64,1024]{1,0:T(8,128)(2,1)} %v_ref.1, bf16[64,8192]{1,0:T(8,128)(2,1)} %g_ref.1, s32[1,2048]{1,0:T(1,128)} %bitcast.1), custom_call_target="tpu_custom_call" | custom-call | tf_op jit(solution)/shard_map/pallas_call | solution.py:428
  61.0 0.0 copy-start.1
  61.0 0.0 copy-start
  61.0 2.7 %convert_element_type.3 = f32[64,8192]{1,0:T(8,128)} convert(bf16[64,8192]{1,0:T(8,128)(2,1)} %get-tuple-element.6) | non-fusion elementwise | flops 524288 | bytes 3145728 | tf_op jit(solution)/shard_map/convert_element_type | solution.py:468
  63.7 0.0 copy-done.1
  63.7 0.7 %copy.10 = f32[64,1024]{1,0:T(8,128)} copy(f32[64,1024]{1,0:T(8,128)S(1)} %copy-done.1) | data formatting | bytes 524288
  64.4 0.0 copy-done
  64.5 0.7 %copy.11 = f32[64,1024]{1,0:T(8,128)} copy(f32[64,1024]{1,0:T(8,128)S(1)} %copy-done) | data formatting | bytes 524288
Async XLA Ops:
  61.0 2.8 %copy-start.1 = (f32[64,1024]{1,0:T(8,128)S(1)}, f32[64,1024]{1,0:T(8,128)}, u32[]{:S(2)}) copy-start(f32[64,1024]{1,0:T(8,128)} %get-tuple-element.13) | copy-start | bytes 786436
  61.0 3.5 %copy-start = (f32[64,1024]{1,0:T(8,128)S(1)}, f32[64,1024]{1,0:T(8,128)}, u32[]{:S(2)}) copy-start(f32[64,1024]{1,0:T(8,128)} %get-tuple-element.14) | copy-start | bytes 786436

commit v2 on v1

v2 whole, which is shorter than its diff:
```python
import functools
import math
import jax
import jax.numpy as jnp
from jax import lax
from jax.experimental import pallas as pl
from jax.experimental.pallas import tpu as pltpu
from jax.sharding import PartitionSpec as P

HD = 128
BACK = 3
SLOTS = 4
CUTS = 8
MESH = pl.DeviceIdType.MESH
NT = (((1,), (1,)), ((), ()))


def flip(v, mask):
    bit = 1
    while bit <= mask:
        if mask & bit:
            v = v + bit * (1 - 2 * ((v // bit) % 2))
        bit *= 2
    return v


def kernel(
    n_ctx, n_head,
    q_ref, k_ref, v_ref, g_ref, doc_ref,
    dq_out, dk_out, dv_out,
    own_buf, qg_buf, dq_buf, kv_buf, kt_buf, acc, bias, red_out, red_in, part_out, tot_in,
    s_buf, p_buf, w_buf, d_buf,
    own_sem, kv_send, kv_recv, in_send, in_recv, up_send, up_recv, last_send, last_recv,
    dq_send, dq_recv, red_send, red_recv, part_send, tot_send, tot_recv,
):
    c = lax.axis_index("ctx")
    h = lax.axis_index("head")
    k = c % 2
    z = c // 2
    n_z = n_ctx // 2
    rows = q_ref.shape[0]
    blk = rows * n_head
    jobs, _, n_st, _, pair, width = qg_buf.shape
    heads = width // HD
    scale = 1.0 / HD**0.5
    has_up, has_down, has_two = z + 1 < n_z, z >= 1, z >= 2

    def at(n, size):
        return pl.ds(pl.multiple_of(n * size, size), size)

    def bit_of(v, j):
        return (v // (1 << j % 2)) % 2

    def dev(dk, dh):
        return (flip(c, dk), flip(h, dh))

    mine = [2 * bit_of(h, j) + k for j in range(jobs)]
    plane = [(dk, dh) for dh in range(n_head) for dk in range(2)]
    others = plane[1:]
    up = ((c + 2) % n_ctx, h)
    down = ((c - 2 + n_ctx) % n_ctx, h)

    def masks(j):
        return [m for m in range(1, n_head) if not m >> j % 2 & 1]

    def place(v, j):
        bit = 1 << j % 2
        return v % bit + v // (2 * bit) * bit

    def head_of(b, o, j):
        bit = 1 << j % 2
        return o % bit + b * bit + o // bit * 2 * bit


    barrier = pltpu.get_barrier_semaphore()
    for to in [dev(*p) for p in others] + [up, down]:
        pl.semaphore_signal(barrier, inc=1, device_id=to, device_id_type=MESH)

    for j in range(jobs):
        for b in range(2):
            for core in range(2):
                head = head_of(b, h // 2, j)
                above = (2 * z + 2 + core) % n_ctx
                pl.semaphore_signal(barrier, inc=1, device_id=(above, head), device_id_type=MESH)

                @pl.when(k == 1)
                def _():
                    far = (2 * z + 4 + core) % n_ctx
                    pl.semaphore_signal(barrier, inc=1, device_id=(far, head), device_id_type=MESH)
    for t in range(2):
        pltpu.make_async_copy((k_ref, v_ref)[t], own_buf.at[t], own_sem.at[t]).start()

    def kv_copy(j, t, p):
        dk, dh = p
        slot = 2 * bit_of(flip(h, dh), j) + flip(k, dk)
        src = own_buf.at[t, :, at(SLOTS * j + slot, HD)]
        dst = kv_buf.at[j, BACK + k, t, at(h, rows)]
        return pltpu.make_async_remote_copy(
            src_ref=src, dst_ref=dst,
            send_sem=kv_send.at[j, dh], recv_sem=kv_recv.at[j, dh],
            device_id=dev(dk, dh), device_id_type=MESH,
        )

    def await_bytes(ref, sem):
        pltpu.make_async_copy(ref, ref, sem).wait()

    def kv_arrived(j, dh):
        if dh == 0:
            await_bytes(kv_buf.at[j, BACK, :, at(h, rows)], kv_recv.at[j, 0])
            for t in range(2):
                kv_buf[j, BACK + k, t, at(h, rows)] = own_buf[t, :, at(SLOTS * j + mine[j], HD)]
        else:
            await_bytes(kv_buf.at[j, BACK : BACK + 2, :, at(flip(h, dh), rows)], kv_recv.at[j, dh])

    def in_copy(j, s, t, dk, db):
        slot = 2 * flip(bit_of(h, j), db) + flip(k, dk)
        src = (q_ref, g_ref)[t].at[:, at((SLOTS * j + slot) * n_st + s, width)]
        dst = qg_buf.at[j, k, s, t, at(bit_of(h, j), rows)]
        arrive = in_recv.at[j, s, k]
        if (dk, db) == (0, 0):
            return pltpu.make_async_copy(src, dst, arrive)
        return pltpu.make_async_remote_copy(
            src_ref=src, dst_ref=dst,
            send_sem=in_send.at[j, db], recv_sem=arrive,
            device_id=dev(dk, db << j % 2), device_id_type=MESH,
        )

    def in_arrived(j, s, kk):
        await_bytes(qg_buf.at[j, kk, s], in_recv.at[j, s, kk])

    def up_copy(j, kk, dh):
        part = kv_buf.at[j, BACK + kk, :, at(flip(h, dh), rows)]
        return pltpu.make_async_remote_copy(
            src_ref=part, dst_ref=kv_buf.at[j, BACK + kk - 2, :, at(flip(h, dh), rows)],
            send_sem=up_send.at[j], recv_sem=up_recv.at[j, kk, dh],
            device_id=up, device_id_type=MESH,
        )

    def last_copy(j, dh):
        return pltpu.make_async_remote_copy(
            src_ref=kv_buf.at[j, 2, :, at(flip(h, dh), rows)], dst_ref=kv_buf.at[j, 0, :, at(flip(h, dh), rows)],
            send_sem=last_send.at[j], recv_sem=last_recv.at[j],
            device_id=up, device_id_type=MESH,
        )

    def dq_send_out(j, s, kk):
        for b in range(2):
            src = dq_buf.at[j, kk, s, pl.ds(b * rows, rows)]
            dst = dq_out.at[:, at((SLOTS * j + mine[j]) * n_st + s, width)]
            here = (k == kk) & (bit_of(h, j) == b)

            @pl.when(jnp.logical_not(here))
            def _():
                pltpu.make_async_remote_copy(
                    src_ref=src, dst_ref=dst,
                    send_sem=dq_send.at[j, (k + kk) % 2], recv_sem=dq_recv.at[j],
                    device_id=(2 * z + kk, h + (1 << j % 2) * (b - bit_of(h, j))), device_id_type=MESH,
                ).start()

            @pl.when(here)
            def _():
                pltpu.make_async_copy(src, dst, dq_recv.at[j]).start()

    def red_copy(j, i, n):
        mask = masks(j)[n]
        return pltpu.make_async_remote_copy(
            src_ref=red_out.at[j, i, :, at(place(flip(h, mask), j), pair)], dst_ref=red_in.at[j, i, n],
            send_sem=red_send.at[j, i], recv_sem=red_recv.at[j, i],
            device_id=(c, flip(h, mask)), device_id_type=MESH,
        )

    group = n_head // 2

    def part_copy(j, i, e):
        return pltpu.make_async_remote_copy(
            src_ref=part_out.at[j, i, :, pl.ds(e * rows, rows)],
            dst_ref=tot_in.at[j, mine[j], group + (1 if i == 0 else 0)],
            send_sem=part_send.at[j, i, e], recv_sem=tot_recv.at[j, mine[j], group + (1 if i == 0 else 0)],
            device_id=((2 * z - BACK + i + n_ctx) % n_ctx, 2 * place(h, j) + e), device_id_type=MESH,
        )

    def tot_copy(j, p):
        dk, dh = p
        return pltpu.make_async_remote_copy(
            src_ref=red_out.at[j, BACK + flip(k, dk), :, at(flip(h, dh), rows)],
            dst_ref=tot_in.at[j, mine[j], place(h, j)],
            send_sem=tot_send.at[j, dk, dh], recv_sem=tot_recv.at[j, mine[j], place(h, j)],
            device_id=dev(dk, dh), device_id_type=MESH,
        )

    def start_kv(j):
        for p in others:
            for t in range(2):
                kv_copy(j, t, p).start()

    def start_in(j, s):
        for db in range(2):
            for dk in range(2):
                for t in range(2):
                    in_copy(j, s, t, dk, db).start()

    tile = HD
    lane = lax.broadcasted_iota(jnp.int32, (8, blk), 1)

    def make_bias(j, kk):
        shift = 1 << j % 2
        block = 2 * z + kk
        docs = jnp.broadcast_to(
            doc_ref[:, pl.ds(pl.multiple_of(block * blk, blk), blk)].astype(jnp.float32), (8, blk)
        )
        first = h - shift * bit_of(h, j)
        query_doc = jnp.zeros((8, blk), jnp.float32)
        for u in range(heads):
            for b in range(2):
                to = (2 * u + b) * rows
                turn = (to - (first + b * shift) * rows + 2 * blk) % blk
                query_doc = jnp.where(lane // rows == 2 * u + b, pltpu.roll(docs, turn, 1), query_doc)
        query_doc = query_doc[:1]
        col = lax.broadcasted_iota(jnp.int32, (tile, blk), 1)
        i = (first + (col // rows) % 2 * shift) * rows + col % rows
        for part in range(4 * blk // tile):
            key_blk = jnp.maximum(block - BACK + part * tile // blk, 0)
            start = pl.multiple_of(key_blk * blk + part * tile % blk, tile)
            key_row = doc_ref[:, pl.ds(start, tile)].astype(jnp.float32)
            key_doc = jnp.transpose(jnp.broadcast_to(key_row, (tile, tile)))
            key_doc = jnp.concatenate([key_doc] * (blk // tile), axis=1)
            row = lax.broadcasted_iota(jnp.int32, (tile, blk), 0) + part * tile
            ok = (row > i) & (row <= i + BACK * blk) & (row + (block - BACK) * blk >= 0)
            ok = ok & (key_doc == query_doc)
            bias[j, kk, pl.ds(part * tile, tile)] = jnp.where(ok, 0.0, -1e30)

    def gather_and_send_up(j):
        for dh in range(n_head):
            kv_arrived(j, dh)

            @pl.when(has_up)
            def _():
                for kk in (1, 0):
                    up_copy(j, kk, dh).start()

            yield

    def fill(j):
        @pl.when(z < 1)
        def _():
            kv_buf[j, 1:3] = jnp.zeros((2,) + kv_buf.shape[2:], kv_buf.dtype)

        @pl.when(z < 2)
        def _():
            kv_buf[j, 0] = jnp.zeros(kv_buf.shape[2:], kv_buf.dtype)

    def wait_down(j):
        @pl.when(has_down)
        def _():
            for dh in range(n_head):
                await_bytes(kv_buf.at[j, 1, :, at(flip(h, dh), rows)], up_recv.at[j, 0, dh])

    def hand_on(j):
        @pl.when(has_down)
        def _():
            for dh in range(n_head):
                await_bytes(kv_buf.at[j, 2, :, at(flip(h, dh), rows)], up_recv.at[j, 1, dh])
                pl.when(has_up)(last_copy(j, dh).start)

    def wait_last(j):
        @pl.when(has_two)
        def _():
            await_bytes(kv_buf.at[j, 0], last_recv.at[j])

    def turn_keys(j, first, last):
        keys = kv_buf[j, first:last, 0].reshape((last - first) * blk, HD)
        kt_buf[j, :, first * blk : last * blk] = jnp.transpose(keys.astype(jnp.float32)).astype(jnp.bfloat16)

    lanes = [slice(a * HD, (a + 1) * HD) for a in range(heads)]
    log_scale = scale * math.log2(math.e)
    fine = 32
    tiles = 4 * blk // fine

    def stacked(j, kk, s, t):
        return jnp.concatenate([qg_buf[j, kk, s, t, :, a] for a in lanes], axis=0)

    def fold(x, op):
        return op(x.reshape(x.shape[0] // 8, 8, blk), axis=0)

    def scores(step, slot, made):
        j, kk, s = step
        q, g = stacked(j, kk, s, 0), stacked(j, kk, s, 1)
        high = None
        for n in range(4):
            s_t = lax.dot_general(kv_buf[j, kk + n, 0], q, NT, preferred_element_type=jnp.float32)
            p_t = lax.dot_general(kv_buf[j, kk + n, 1], g, NT, preferred_element_type=jnp.float32)
            for m in range(blk // fine):
                span, part = pl.ds(n * blk + m * fine, fine), slice(m * fine, (m + 1) * fine)
                one = s_t[part] + bias[j, kk, span]
                s_buf[slot][span] = one
                p_buf[slot][span] = p_t[part]
                one = fold(one, jnp.max)
                high = one if high is None else jnp.maximum(high, one)
                yield
        made["top"] = jnp.max(high, axis=0, keepdims=True)

    def exponentials(slot, made):
        top = made["top"]
        total = None
        for n in range(tiles):
            span = pl.ds(n * fine, fine)
            e_t = jnp.exp2((s_buf[slot][span] - top) * log_scale)
            s_buf[slot][span] = e_t
            one = fold(e_t, jnp.sum)
            total = one if total is None else total + one
            yield
        made["inverse"] = 1.0 / jnp.sum(total, axis=0, keepdims=True)

    def weights(slot, to, made):
        inverse = made["inverse"]
        total = None
        for n in range(tiles):
            span = pl.ds(n * fine, fine)
            w_t = s_buf[slot][span] * inverse
            s_buf[slot][span] = w_t
            w_bf = w_t.astype(jnp.bfloat16)
            w_buf[to][span] = w_bf
            one = fold(w_bf.astype(jnp.float32) * p_buf[slot][span], jnp.sum)
            total = one if total is None else total + one
            yield
        made["delta"] = jnp.sum(total, axis=0, keepdims=True)

    def differences(slot, to, made):
        delta = made["delta"]
        for n in range(tiles):
            span = pl.ds(n * fine, fine)
            d_buf[to][span] = (s_buf[slot][span] * (p_buf[slot][span] - delta)).astype(jnp.bfloat16)
            yield

    def gradients(step, slot, slot_w):
        j, kk, s = step
        q, g = stacked(j, kk, s, 0), stacked(j, kk, s, 1)
        for n in range(4):
            span = pl.ds(n * blk, blk)
            for t, left, right in ((1, w_buf[slot_w], g), (0, d_buf[slot], q)):
                more = jnp.dot(left[span], right, preferred_element_type=jnp.float32)
                for m in range(0, blk, 2 * fine):
                    acc[j, kk + n, t, pl.ds(m, 2 * fine)] += more[m : m + 2 * fine]
                    yield
        keys_t = kt_buf[j, :, kk * blk : (kk + 4) * blk]
        dq_t = jnp.dot(keys_t, d_buf[slot][...], preferred_element_type=jnp.float32)
        dq = jnp.transpose(dq_t * scale).astype(jnp.bfloat16)
        for n, a in enumerate(lanes):
            dq_buf[j, kk, s, :, a] = dq[n * pair : (n + 1) * pair]

    def in_turns(pieces):
        pieces = list(pieces)
        while pieces:
            pieces = [p for p in pieces if next(p, "end") != "end"]

    need = (has_two, has_down, has_down)

    def round_out(j, i):
        red_out[j, i, 0] = (acc[j, i, 0] * scale).astype(jnp.bfloat16)
        red_out[j, i, 1] = acc[j, i, 1].astype(jnp.bfloat16)

    def share(j, i):
        round_out(j, i)

        @pl.when(need[i])
        def _():
            for n in range(len(masks(j))):
                red_copy(j, i, n).start()

    def send_part(j, i):
        @pl.when(need[i])
        def _():
            await_bytes(red_in.at[j, i], red_recv.at[j, i])
            mine_here = at(place(h, j), pair)
            sums = [acc[j, i, 0, mine_here] * scale, acc[j, i, 1, mine_here]]
            for t in range(2):
                for n in range(len(masks(j))):
                    sums[t] = sums[t] + red_in[j, i, n, t].astype(jnp.float32)
                part_out[j, i, t] = sums[t].astype(jnp.bfloat16)
            for e in range(2):
                part_copy(j, i, e).start()

    def send_own(j):
        for kk in range(2):
            round_out(j, BACK + kk)
        for p in others:
            tot_copy(j, p).start()
        tot_in[j, mine[j], place(h, j)] = red_out[j, BACK + k, :, at(h, rows)]

    for j in range(jobs):
        fill(j)
        acc[j] = jnp.zeros(acc.shape[1:], acc.dtype)
        for kk in range(2):
            make_bias(j, kk)

    pl.semaphore_wait(barrier, len(others) + 2 + 6 * jobs)
    for t in range(2):
        await_bytes(own_buf.at[t], own_sem.at[t])
    start_kv(0)
    start_in(0, 0)
    start_in(0, 1)
    for j in range(1, jobs):
        start_kv(j)
    for j in range(jobs):
        @pl.loop(2 if j == 0 else 0, n_st)
        def _(s):
            start_in(j, s)

    for _ in gather_and_send_up(0):
        pass
    hand_on(0)
    wait_down(0)
    turn_keys(0, 1, 5)

    steps = []
    half = n_st // 2
    for j in range(jobs):
        if j == 0:
            order = [(kk, s) for kk in (1, 0) for s in range(half)] + [(kk, s) for s in range(half, n_st) for kk in (1, 0)]
        else:
            order = [(1, s) for s in range(half)] + [(0, s) for s in range(n_st)] + [(1, s) for s in range(half, n_st)]
        steps += [(j, kk, s) for kk, s in order]
    per_job = 2 * n_st

    def before(n):
        j, first = n // per_job, n % per_job
        if j > 0 and first == 0:
            wait_down(j)
            turn_keys(j, 1, 5)
        if first == half:
            wait_last(j)
            turn_keys(j, 0, 1)
        if first == 1 and j + 1 < jobs:
            for _ in gather_and_send_up(j + 1):
                pass
        if first == per_job - 2 and j + 1 < jobs:
            hand_on(j + 1)
        in_arrived(*steps[n][:1], steps[n][2], steps[n][1])

    def after(n):
        j, first = n // per_job, n % per_job
        dq_send_out(j, steps[n][2], steps[n][1])
        last = j == jobs - 1
        if j > 0 and first == per_job // 2:
            send_part(j - 1, 0)
            send_part(j - 1, 1)
        if j > 0 and first == half + n_st - 1:
            share(j, 0)
        if j > 0 and first == per_job - 2:
            send_part(j - 1, 2)
        if first == per_job - 1:
            for i in range(1 if j > 0 else 0, BACK):
                share(j, i)
            send_own(j)
            if last:
                for i in range(BACK):
                    send_part(j, i)

    made = [{} for _ in steps]
    for n in range(len(steps) + 4):
        pieces = []
        if n < len(steps):
            before(n)
        if 0 <= n - 4:
            pieces.append(gradients(steps[n - 4], n % 2, (n - 4) % 3))
        if n < len(steps):
            pieces.append(scores(steps[n], n % 4, made[n]))
        if 0 <= n - 1 < len(steps):
            pieces.append(exponentials((n - 1) % 4, made[n - 1]))
        if 0 <= n - 2 < len(steps):
            pieces.append(weights((n - 2) % 4, (n - 2) % 3, made[n - 2]))
        if 0 <= n - 3 < len(steps):
            pieces.append(differences((n - 3) % 4, (n - 3) % 2, made[n - 3]))
        in_turns(pieces)
        if 0 <= n - 4:
            after(n - 4)

    for j in range(jobs):
        for slot in range(SLOTS):
            n = SLOTS * j + slot
            for o in range(group):
                @pl.when((mine[j] != slot) | (place(h, j) != o))
                def _():
                    await_bytes(tot_in.at[j, slot, o], tot_recv.at[j, slot, o])

            for far, cond in ((0, has_up), (1, (z + 2 < n_z) & (k == 1))):
                @pl.when(cond)
                def _():
                    await_bytes(tot_in.at[j, slot, group + far], tot_recv.at[j, slot, group + far])

                @pl.when(jnp.logical_not(cond))
                def _():
                    tot_in[j, slot, group + far] = jnp.zeros(tot_in.shape[3:], tot_in.dtype)

            for t in range(2):
                total = tot_in[j, slot, 0, t].astype(jnp.float32)
                for o in range(1, group + 2):
                    total = total + tot_in[j, slot, o, t].astype(jnp.float32)
                (dk_out, dv_out)[t][:, n * HD : (n + 1) * HD] = total

    for j in range(jobs):
        await_bytes(dq_buf.at[j, 0], in_send.at[j, 0])
        await_bytes(qg_buf.at[j, 0], in_send.at[j, 1])
        await_bytes(dq_buf.at[j, 0, :, pl.ds(0, rows)], dq_send.at[j, 0])
        await_bytes(dq_buf.at[j, 0], dq_send.at[j, 1])
        await_bytes(qg_buf.at[j, 0], dq_recv.at[j])
        await_bytes(kv_buf.at[j, 0, :, pl.ds(0, rows)], kv_send.at[j, 0])
        for dh in range(1, n_head):
            await_bytes(kv_buf.at[j, 0:2, :, pl.ds(0, rows)], kv_send.at[j, dh])
        for p in others:
            tot_copy(j, p).wait_send()

        for i in range(BACK):
            @pl.when(need[i])
            def _():
                await_bytes(red_in.at[j, i], red_send.at[j, i])
                for e in range(2):
                    part_copy(j, i, e).wait_send()

        @pl.when(has_up)
        def _():
            await_bytes(kv_buf.at[j, 0:2], up_send.at[j])

        @pl.when(has_up & has_down)
        def _():
            await_bytes(kv_buf.at[j, 0], last_send.at[j])


def widen(*refs):
    src, dst, near, wide, (get, put) = refs[:3], refs[3:6], refs[6:9], refs[9:12], refs[12:]
    step = src[0].shape[1] // CUTS
    pieces = [(0, pl.ds(n * step, step)) for n in range(CUTS)] + [(n, pl.ds(0, src[n].shape[1])) for n in (1, 2)]
    reads = [pltpu.make_async_copy(src[a].at[:, s], near[a].at[:, s], get.at[n]) for n, (a, s) in enumerate(pieces)]
    writes = [pltpu.make_async_copy(wide[a].at[:, s], dst[a].at[:, s], put.at[n]) for n, (a, s) in enumerate(pieces)]
    for read in reads:
        read.start()
    for (a, s), read, write in zip(pieces, reads, writes):
        read.wait()
        wide[a][:, s] = near[a][:, s].astype(jnp.float32)
        write.start()
    for write in writes:
        write.wait()


def body(queries, keys, values, out_grad, doc_ids):
    n_ctx, n_head = lax.axis_size("ctx"), lax.axis_size("head")
    rows, q_cols = queries.shape
    kv_cols = keys.shape[1]
    blk = rows * n_head
    jobs = kv_cols // HD // SLOTS
    group = q_cols // kv_cols
    heads = n_head // 2
    n_st = group // heads
    pair = 2 * rows
    win = BACK + 2
    bf, f32, dma = jnp.bfloat16, jnp.float32, pltpu.SemaphoreType.DMA
    far = pl.BlockSpec(memory_space=pl.ANY)
    near = pl.BlockSpec(memory_space=pltpu.VMEM)
    dq, dk, dv = pl.pallas_call(
        functools.partial(kernel, n_ctx, n_head),
        out_shape=(
            jax.ShapeDtypeStruct((rows, q_cols), bf),
            jax.ShapeDtypeStruct((rows, kv_cols), f32),
            jax.ShapeDtypeStruct((rows, kv_cols), f32),
        ),
        in_specs=[far, far, far, far, near],
        out_specs=(far, near, near),
        scratch_shapes=[
            pltpu.VMEM((2, rows, kv_cols), bf),
            pltpu.VMEM((jobs, 2, n_st, 2, pair, heads * HD), bf),
            pltpu.VMEM((jobs, 2, n_st, pair, heads * HD), bf),
            pltpu.VMEM((jobs, win, 2, blk, HD), bf),
            pltpu.VMEM((jobs, HD, win * blk), bf),
            pltpu.VMEM((jobs, win, 2, blk, HD), f32),
            pltpu.VMEM((jobs, 2, 4 * blk, blk), f32),
            pltpu.VMEM((jobs, win, 2, blk, HD), bf),
            pltpu.VMEM((jobs, BACK, n_head // 2 - 1, 2, pair, HD), bf),
            pltpu.VMEM((jobs, BACK, 2, pair, HD), bf),
            pltpu.VMEM((jobs, SLOTS, n_head // 2 + 2, 2, rows, HD), bf),
            (pltpu.VMEM((4 * blk, blk), f32),) * 4,
            (pltpu.VMEM((4 * blk, blk), f32),) * 4,
            (pltpu.VMEM((4 * blk, blk), bf),) * 3,
            (pltpu.VMEM((4 * blk, blk), bf),) * 2,
            dma((2,)),
            dma((jobs, n_head)),
            dma((jobs, n_head)),
            dma((jobs, 2)),
            dma((jobs, n_st, 2)),
            dma((jobs,)),
            dma((jobs, 2, n_head)),
            dma((jobs,)),
            dma((jobs,)),
            dma((jobs, 2)),
            dma((jobs,)),
            dma((jobs, BACK)),
            dma((jobs, BACK)),
            dma((jobs, BACK, 2)),
            dma((jobs, 2, n_head)),
            dma((jobs, SLOTS, n_head // 2 + 2)),
        ],
        compiler_params=pltpu.CompilerParams(
            collective_id=0, has_side_effects=True, vmem_limit_bytes=56 * 2**20
        ),
    )(queries, keys, values, out_grad, doc_ids.reshape(1, -1))
    outs = [jax.ShapeDtypeStruct(x.shape, f32) for x in (dq, dk, dv)]
    return pl.pallas_call(
        widen,
        out_shape=outs,
        in_specs=[far] * 3,
        out_specs=[far] * 3,
        scratch_shapes=[
            *[pltpu.VMEM(x.shape, x.dtype) for x in (dq, dk, dv)],
            *[pltpu.VMEM(x.shape, f32) for x in (dq, dk, dv)],
            dma((CUTS + 2,)),
            dma((CUTS + 2,)),
        ],
    )(dq, dk, dv)


def solution(mesh):
    split = P(("ctx", "head"), None)
    return jax.shard_map(
        body,
        mesh=mesh,
        in_specs=(split, split, split, split, P()),
        out_specs=(split, split, split),
        check_vma=False,
    )
```

time: 65.7 us -> 55 us (0.84)
  Pallas kernels: 60.3 us -> 53.8 us
  other arithmetic: 2.74 us -> 0 us
  local copies, waits for them, and re-layouts: 1.41 us -> 0 us
    pallas_call x1, Pallas kernels: 60.3 us -> 51.2 us  [body(): pl.pallas_call(functools.partial(kernel, n_ctx, n_head), out_shape=(jax.S...]
    convert_element_type x1 -> x0, other arithmetic: 2.74 us -> none  [body(): return (dq.astype(f32), dk, dv)]
    pallas_call x0 -> x1, Pallas kernels: none -> 2.58 us  [body(): pl.pallas_call(widen, out_shape=outs, in_specs=[far] * 3, out_specs=[far]...]
    unnamed x6 -> x0, local copies, waits for them, and re-layouts: 1.41 us -> none
where the time goes in v2:
time: 55 us; the launch traced here: 54.6 us
  Pallas kernels  53.8 us (98%)
  between operations  0.82 us (1%)
    pallas_call x1, Pallas kernels, body(): pl.pallas_call(functools.partial(kernel, n_ctx, n_head), out_shape=(jax.S...  51.2 us
    pallas_call x1, Pallas kernels, body(): pl.pallas_call(widen, out_shape=outs, in_specs=[far] * 3, out_specs=[far]...  2.58 us

profile of v2, /device:TPU:1, one launch (start us, length us, event | category | flops | bytes accessed | tf_op | source)
XLA Modules:
  0.0 54.6 jit_solution(611041548004716021)
XLA Ops:
  0.6 51.2 %shard_map.76 = (bf16[64,8192]{1,0:T(8,128)(2,1)}, f32[64,1024]{1,0:T(8,128)}, f32[64,1024]{1,0:T(8,128)}) custom-call(bf16[64,8192]{1,0:T(8,128)(2,1)} %q_ref.1, bf16[64,1024]{1,0:T(8,128)(2,1)} %k_ref.1, bf16[64,1024]{1,0:T(8,128)(2,1)} %v_ref.1, bf16[64,8192]{1,0:T(8,128)(2,1)} %g_ref.1, s32[1,2048]{1,0:T(1,128)} %bitcast.1), custom_call_target="tpu_custom_call" | custom-call | tf_op jit(solution)/shard_map/pallas_call | solution.py:559
  51.8 2.6 %shard_map.77 = (f32[64,8192]{1,0:T(8,128)}, f32[64,1024]{1,0:T(8,128)}, f32[64,1024]{1,0:T(8,128)}) custom-call(bf16[64,8192]{1,0:T(8,128)(2,1)} %get-tuple-element.6.refs_0_, f32[64,1024]{1,0:T(8,128)} %get-tuple-element.7.refs_1_, f32[64,1024]{1,0:T(8,128)} %get-tuple-element.8.refs_2_), custom_call_target="tpu_custom_call" | custom-call | tf_op jit(solution)/shard_map/pallas_call | solution.py:606
